TPU v7x, 32 devices: a whole 2x2x4 slice. The times are simulated.
32 devices in a mesh: seq: 8 (over z, y), mp: 4 (over x, core).
Axes of the slice: x: 2, y: 2, z: 4, core: 2. Of those that a mesh axis runs over, the one named last changes fastest.
Arguments:
- hidden_in: bfloat16 [2, 1024, 2048], P(None, 'seq'), may hold values from -6 to 6
- attn_gain: float32 [2048], replicated, may hold values from 0.1 to 1.9
- q_weight: bfloat16 [2048, 2048], P(None, 'mp'), may hold values from -0.125 to 0.125
- q_bias: float32 [2048], P('mp'), may hold values from -60 to 60
- k_weight: bfloat16 [2048, 256], replicated, may hold values from -0.125 to 0.125
- k_bias: float32 [256], replicated, may hold values from -60 to 60
- v_weight: bfloat16 [2048, 256], replicated, may hold values from -0.125 to 0.125
- v_bias: float32 [256], replicated, may hold values from -3 to 3
- o_weight: bfloat16 [2048, 2048], P('mp'), may hold values from -0.125 to 0.125
- mlp_gain: float32 [2048], replicated, may hold values from 0.1 to 1.9
- gate_weight: bfloat16 [2048, 5632], P('seq', 'mp'), may hold values from -0.125 to 0.125
- up_weight: bfloat16 [2048, 5632], P('seq', 'mp'), may hold values from -0.125 to 0.125
- down_weight: bfloat16 [2048, 5632], P('seq', 'mp'), may hold values from -0.078125 to 0.078125
- lengths: int32 [2], replicated, may hold values from 512 to 1024
Outputs:
- layer_out: bfloat16 [2, 1024, 2048], P(None, 'seq', 'mp')
- influence: float32 [2, 1024], P(None, 'seq')
- score: float32 [2], replicated
Inputs may be any that keep to these rules, and one draw needn't show every extreme that they name: `lengths`: tokens at positions 512 and later may be invalid.
All inputs are finite; a program needn't handle non-finite values.
Results may differ from a plain program's by a relative error of at most 0.02.
The roundings to bfloat16 on the way count: a program that leaves them out, or rounds other values in their place, can miss the bound.
Values may be sent and summed in bfloat16 or wider, within the bound.
A program may use at most 192 MiB of HBM per device.

v0:
```python
import jax
import jax.numpy as jnp
from jax import lax
from jax.sharding import PartitionSpec as P

HEADS = 16
KV_HEADS = 2
HEAD = 128
rope_base = 1000000.0
norm_eps = 1e-06
masked_score = -1e30


def rms_scale(values, gain):
    widened = values.astype(jnp.float32)
    factor = lax.rsqrt(jnp.mean(widened * widened, axis=-1, keepdims=True) + norm_eps)
    return (widened * factor * gain).astype(jnp.bfloat16)


def rotate(values, positions):
    head_width = values.shape[-1]
    half_width = head_width // 2
    inv_freq = rope_base ** (-(jnp.arange(half_width, dtype=jnp.float32) * 2.0) / head_width)
    angles = positions.astype(jnp.float32)[:, None] * inv_freq[None, :]
    angles = jnp.concatenate([angles, angles], axis=-1)
    first_part = values[..., :half_width]
    second_part = values[..., half_width:]
    turned = jnp.concatenate([-second_part, first_part], axis=-1)
    return values * jnp.cos(angles) + turned * jnp.sin(angles)


def attend_update(state, queries, first_pos, key_piece, value_piece):
    run_max, run_sum, run_acc = state
    score_scale = queries.shape[-1] ** (-0.5)
    query_pos = first_pos + jnp.arange(queries.shape[2], dtype=jnp.int32)
    key_pos = jnp.arange(key_piece.shape[1], dtype=jnp.int32)
    scores = (
        jnp.einsum("shqd,skd->shqk", queries, key_piece, preferred_element_type=jnp.float32)
        * score_scale
    )
    allowed = key_pos[None, :] <= query_pos[:, None]
    scores = jnp.where(allowed, scores, masked_score)
    new_max = jnp.maximum(run_max, jnp.max(scores, axis=-1))
    weights = jnp.where(allowed, jnp.exp(scores - new_max[..., None]), 0.0)
    new_sum = jnp.sum(weights, axis=-1)
    mixed = jnp.einsum(
        "shqk,skd->shqd",
        weights.astype(jnp.bfloat16),
        value_piece,
        preferred_element_type=jnp.float32,
    )
    return (new_max, new_sum, mixed)


def local(
    hidden_in,
    attn_gain,
    q_weight,
    q_bias,
    k_weight,
    k_bias,
    v_weight,
    v_bias,
    o_weight,
    mlp_gain,
    gate_weight,
    up_weight,
    down_weight,
    lengths,
):
    seqs_n, tok_n, width = hidden_in.shape
    seq_rank = lax.axis_index("seq")
    mp_devices = lax.axis_size("mp")
    mp_rank = lax.axis_index("mp")
    heads_here = q_weight.shape[1] // HEAD
    group_size = HEADS // KV_HEADS
    kv_index = mp_rank * heads_here // group_size
    flat_in = hidden_in.reshape(seqs_n * tok_n, width)
    normed = rms_scale(flat_in, attn_gain)
    query_all = jnp.dot(normed, q_weight, preferred_element_type=jnp.float32) + q_bias
    key_cols = lax.dynamic_slice_in_dim(k_weight, kv_index * HEAD, HEAD, 1)
    value_cols = lax.dynamic_slice_in_dim(v_weight, kv_index * HEAD, HEAD, 1)
    key_shift = lax.dynamic_slice_in_dim(k_bias, kv_index * HEAD, HEAD, 0)
    value_shift = lax.dynamic_slice_in_dim(v_bias, kv_index * HEAD, HEAD, 0)
    key_all = jnp.dot(normed, key_cols, preferred_element_type=jnp.float32) + key_shift
    value_rows = (
        jnp.dot(normed, value_cols, preferred_element_type=jnp.float32) + value_shift
    ).astype(jnp.bfloat16)
    positions = seq_rank * tok_n + jnp.arange(tok_n, dtype=jnp.int32)
    rotated_q = rotate(
        query_all.reshape(seqs_n, tok_n, heads_here, HEAD).transpose(0, 2, 1, 3), positions
    ).astype(jnp.bfloat16)
    rotated_k = rotate(key_all.reshape(seqs_n, tok_n, HEAD), positions).astype(jnp.bfloat16)
    value_rows = value_rows.reshape(seqs_n, tok_n, HEAD)
    query_sets = ((rotated_q, seq_rank * tok_n),)
    initial = tuple(
        (
            (
                jnp.full(entry[0].shape[:3], masked_score, jnp.float32),
                jnp.zeros(entry[0].shape[:3], jnp.float32),
                jnp.zeros(entry[0].shape, jnp.float32),
            )
            for entry in query_sets
        )
    )
    key_start = jnp.int32(0)
    key_piece = lax.all_gather(rotated_k, "seq", axis=1, tiled=True)
    value_piece = lax.all_gather(value_rows, "seq", axis=1, tiled=True)
    updated = []
    for state, query_entry in zip(initial, query_sets):
        queries, first_pos = query_entry
        last_pos = first_pos + queries.shape[2] - 1

        def run_update(current):
            return attend_update(current, queries, first_pos, key_piece, value_piece)

        def keep_state(current):
            return current

        updated.append(lax.cond(key_start <= last_pos, run_update, keep_state, state))
    results = tuple(updated)
    finished = [(entry[2] / entry[1][..., None]).astype(jnp.bfloat16) for entry in results]
    attn = finished[0]
    attn = attn.transpose(0, 2, 1, 3).reshape(seqs_n * tok_n, heads_here * HEAD)
    projected = jnp.dot(attn, o_weight, preferred_element_type=jnp.float32)
    quarter = width // mp_devices
    own_in = lax.dynamic_slice_in_dim(flat_in, mp_rank * quarter, quarter, 1)
    summed = lax.psum(projected.astype(jnp.bfloat16), "mp").astype(jnp.float32)
    residual = (flat_in.astype(jnp.float32) + summed).astype(jnp.bfloat16)
    resid_part = lax.dynamic_slice_in_dim(residual, mp_rank * quarter, quarter, 1)
    mlp_in = rms_scale(residual, mlp_gain)
    gate_sum = jnp.dot(
        mlp_in,
        lax.all_gather(gate_weight, "seq", axis=0, tiled=True),
        preferred_element_type=jnp.float32,
    )
    up_sum = jnp.dot(
        mlp_in,
        lax.all_gather(up_weight, "seq", axis=0, tiled=True),
        preferred_element_type=jnp.float32,
    )
    activated = (jax.nn.silu(gate_sum) * up_sum).astype(jnp.bfloat16)
    down_part = lax.dot_general(
        activated,
        lax.all_gather(down_weight, "seq", axis=0, tiled=True),
        (((1,), (1,)), ((), ())),
        preferred_element_type=jnp.float32,
    )
    mlp_share = lax.psum_scatter(
        down_part.astype(jnp.bfloat16), "mp", scatter_dimension=1, tiled=True
    ).astype(jnp.float32)
    layer_part = (resid_part.astype(jnp.float32) + mlp_share).astype(jnp.bfloat16)
    in_share = own_in.astype(jnp.float32)
    out_share = layer_part.astype(jnp.float32)
    cross_part = jnp.sum(in_share * out_share, axis=-1).reshape(seqs_n, tok_n)
    out_part = jnp.sum(out_share * out_share, axis=-1).reshape(seqs_n, tok_n)
    cross, out_norm = lax.psum((cross_part, out_part), "mp")
    in_wide = flat_in.astype(jnp.float32)
    in_norm = jnp.sum(in_wide * in_wide, axis=-1).reshape(seqs_n, tok_n)
    cosine = cross / jnp.sqrt((in_norm + norm_eps) * (out_norm + norm_eps))
    valid = positions[None, :] < lengths[:, None]
    influence = jnp.where(valid, 1.0 - cosine, 0.0)
    seq_total = lax.psum(jnp.sum(influence, axis=1), "seq")
    score = seq_total / lengths.astype(jnp.float32)
    return (layer_part.reshape(seqs_n, tok_n, quarter), influence, score)


def solution(mesh):
    placed = (
        P(None, "seq", None),
        P(),
        P(None, "mp"),
        P("mp"),
        P(),
        P(),
        P(),
        P(),
        P("mp", None),
        P(),
        P("seq", "mp"),
        P("seq", "mp"),
        P("seq", "mp"),
        P(),
    )
    return jax.shard_map(
        local,
        mesh=mesh,
        in_specs=placed,
        out_specs=(P(None, "seq", "mp"), P(None, "seq"), P()),
        check_vma=False,
    )
```

profile of v0, /device:TPU:0, one launch (start us, length us, event | category | flops | bytes accessed | tf_op | source)
XLA Modules:
  0.0 447.5 jit_solution(1680391220494171423)
XLA Ops:
  8.0 0.0 copy-start
  8.0 0.0 all-reduce.3.cloned.1.call-start
  8.1 1.6 multiply_reduce_fusion
  9.8 0.0 copy-start.4
  9.8 0.8 dynamic_slice.19
  10.6 1.5 fusion.14
  12.2 0.0 copy-done.4
  12.2 0.0 copy-start.9
  12.2 0.4 convolution_add_fusion.2
  12.6 0.0 copy-start.8
  12.6 0.7 slice_negate_fusion.1
  13.3 0.1 broadcast_multiply_fusion
  13.4 0.3 fusion.36
  13.8 1.2 fusion.34
  15.0 35.3 %all_gather.15 = bf16[2,1024,128]{2,1,0:T(8,128)(2,1)} all-gather(bf16[2,128,128]{2,1,0:T(8,128)(2,1)S(1)} %fusion.34), channel_id=1, replica_groups=mesh['seq'=8,'mp'=4] {'seq'}, dimensions={1}, use_global_device_ids=true | all-gather | bytes 589824 | tf_op jit(solution)/shard_map/all_gather | solution.py:107
  50.2 0.0 copy-done.9
  50.2 0.1 dynamic_slice.21
  50.3 1.5 fusion.19
  51.8 33.2 %all_gather.16 = bf16[2,1024,128]{2,1,0:T(8,128)(2,1)} all-gather(bf16[2,128,128]{2,1,0:T(8,128)(2,1)S(1)} %bitcast.49), channel_id=1, replica_groups=mesh['seq'=8,'mp'=4] {'seq'}, dimensions={1}, use_global_device_ids=true | all-gather | bytes 589824 | tf_op jit(solution)/shard_map/all_gather | solution.py:108
  85.0 0.0 copy-done.8
  85.0 0.0 copy-done.6
  85.0 1.5 convolution_add_fusion
  86.5 1.2 reshape.194
  87.8 0.0 copy-start.2
  87.8 1.2 slice_negate_fusion
  88.9 1.4 fusion.23
  90.4 0.0 copy-done.2
  90.4 3.7 conditional.1
  90.4 0.1 iota_compare_fusion
  90.5 0.0 copy-start.3
  90.5 0.9 fusion
  91.5 0.1 copy-done.3
  91.6 1.1 fusion.3
  92.7 1.3 fusion.2
  94.0 0.2 fusion.32
  94.3 0.2 copy.19
  94.5 0.0 copy-done
  94.5 1.7 convolution_convert_fusion
  96.2 0.0 all-reduce.3.cloned.1.call-update
  96.2 0.0 all-gather.4.cloned.1.call-start
  96.2 0.5 all-gather.4.cloned.1.call-update
  96.8 0.0 all-gather.6.cloned.1.call-start
  96.8 0.5 all-gather.6.cloned.1.call-update
  97.4 0.0 copy-start.7
  97.4 0.0 all-gather.8.cloned.1.call-start
  97.4 0.5 all-gather.8.cloned.1.call-update
  97.9 0.2 reduce-scatter.2.cloned.1.call-start
  98.2 35.9 %all-reduce.3.cloned.1.call-done = bf16[256,2048]{1,0:T(8,128)(2,1)} async-done(((bf16[256,2048]{1,0:T(8,128)(2,1)}), bf16[256,2048]{1,0:T(8,128)(2,1)}) %all-reduce.3.cloned.1.call-update) | async-done | bytes 1048592 | tf_op jit(solution)/shard_map/psum | solution.py:128
  134.1 0.0 copy-done.1
  134.1 2.6 fusion.16
  136.7 55.5 %all-gather.4.cloned.1.call-done = bf16[2048,1408]{1,0:T(8,128)(2,1)} async-done(((bf16[256,1408]{1,0:T(8,128)(2,1)}), bf16[2048,1408]{1,0:T(8,128)(2,1)}) %all-gather.4.cloned.1.call-update) | async-done | bytes 5767184 | tf_op jit(solution)/shard_map/all_gather | solution.py:134
  192.2 0.0 copy-done.7
  192.2 6.0 %fusion.28 = f32[256,1408]{1,0:T(8,128)} fusion(bf16[2048,1408]{1,0:T(8,128)(2,1)} %all-gather.4.cloned.1.call-done, bf16[256,2048]{1,0:T(8,128)(2,1)} %get-tuple-element.27, f32[2048]{0:T(1024)S(1)} %copy-done.7, f32[256]{0:T(256)S(1)} %add_rsqrt_fusion), kind=kOutput, calls=%fused_computation.48 | convolution fusion | flops 1478492160 | bytes 8266752 | tf_op jit(solution)/shard_map/dot_general | solution.py:132
  198.2 86.4 %all-gather.6.cloned.1.call-done = bf16[2048,1408]{1,0:T(8,128)(2,1)} async-done(((bf16[256,1408]{1,0:T(8,128)(2,1)}), bf16[2048,1408]{1,0:T(8,128)(2,1)}) %all-gather.6.cloned.1.call-update) | async-done | bytes 5767184 | tf_op jit(solution)/shard_map/all_gather | solution.py:139
  284.6 92.4 %all-gather.8.cloned.1.call-done = bf16[2048,1408]{1,0:T(8,128)(2,1)} async-done(((bf16[256,1408]{1,0:T(8,128)(2,1)}), bf16[2048,1408]{1,0:T(8,128)(2,1)}) %all-gather.8.cloned.1.call-update) | async-done | bytes 5767184 | tf_op jit(solution)/shard_map/all_gather | solution.py:145
  376.9 9.5 %convolution_convert_fusion.1 = bf16[256,2048]{1,0:T(8,128)(2,1)} fusion(bf16[2048,1408]{1,0:T(8,128)(2,1)} %all-gather.8.cloned.1.call-done, bf16[2048,1408]{1,0:T(8,128)(2,1)} %all-gather.6.cloned.1.call-done, f32[256,1408]{1,0:T(8,128)} %fusion.28, bf16[256,2048]{1,0:T(8,128)(2,1)} %get-tuple-element.27, f32[2048]{0:T(1024)S(1)} %copy-done.7, ...), kind=kOutput, calls=%fused_computation.23 | convolution fusion | flops 2957574144 | bytes 15082496 | tf_op jit(solution)/shard_map/dot_general | solution.py:143
  386.4 0.0 reduce-scatter.2.cloned.1.call-update
  386.5 23.1 %reduce-scatter.2.cloned.1.call-done = bf16[256,512]{1,0:T(8,128)(2,1)} async-done(((bf16[256,2048]{1,0:T(8,128)(2,1)}), bf16[256,512]{1,0:T(8,128)(2,1)}) %reduce-scatter.2.cloned.1.call-update) | async-done | bytes 262160 | tf_op jit(solution)/shard_map/reduce_scatter | solution.py:149
  409.5 1.8 fusion.21
  411.4 5.7 %all-reduce = (f32[2,128]{1,0:T(2,128)S(1)}, f32[2,128]{1,0:T(2,128)S(1)}) all-reduce(f32[2,128]{1,0:T(2,128)S(1)} %bitcast.52, f32[2,128]{1,0:T(2,128)S(1)} %bitcast.51), channel_id=1, replica_groups=mesh['seq'=8,'mp'=4] {'mp'}, use_global_device_ids=true, to_apply=%region_9.10 | all-reduce | flops 512 | bytes 4096 | tf_op jit(solution)/shard_map/psum | solution.py:157
  417.1 0.0 copy-done.5
  417.1 0.7 fusion.41
  417.8 21.5 %psum.31 = f32[2]{0:T(128)S(1)} all-reduce(f32[2]{0:T(128)S(1)} %get-tuple-element.23), channel_id=1, replica_groups=mesh['seq'=8,'mp'=4] {'seq'}, use_global_device_ids=true, to_apply=%region_13.14 | all-reduce | flops 2 | bytes 16 | tf_op jit(solution)/shard_map/psum | solution.py:163
  439.4 0.5 convert_divide_fusion
  (11 shorter events, 0.1 us)
Async XLA Ops:
  8.0 86.5 %copy-start = (bf16[512,2048]{1,0:T(8,128)(2,1)S(1)}, bf16[512,2048]{1,0:T(8,128)(2,1)}, u32[]{:S(2)}) copy-start(bf16[512,2048]{1,0:T(8,128)(2,1)} %param.24) | copy-start | bytes 6291460
  8.0 126.1 %all-reduce.3.cloned.1.call-start = ((), (), s32[]{:S(2)}) async-start(), calls=%async_computation.1 | async-start | bytes 2097152 | tf_op jit(solution)/shard_map/psum | solution.py:128
  9.8 2.4 copy-start.4
  12.2 38.1 %copy-start.9 = (f32[256]{0:T(256)S(1)}, f32[256]{0:T(256)}, u32[]{:S(2)}) copy-start(f32[256]{0:T(256)} %param.23) | copy-start | bytes 3076
  12.6 72.4 %copy-start.8 = (f32[512]{0:T(512)S(1)}, f32[512]{0:T(512)}, u32[]{:S(2)}) copy-start(f32[512]{0:T(512)} %param.19) | copy-start | bytes 6148
  13.3 71.7 %copy-start.6 = (bf16[2048,512]{1,0:T(8,128)(2,1)S(1)}, bf16[2048,512]{1,0:T(8,128)(2,1)}, u32[]{:S(2)}) copy-start(bf16[2048,512]{1,0:T(8,128)(2,1)} %param.18) | copy-start | bytes 6291460
  87.8 2.6 copy-start.2
  90.5 1.0 copy-start.3
  96.2 38.0 %copy-start.1 = (bf16[2,128,2048]{2,1,0:T(8,128)(2,1)S(1)}, bf16[2,128,2048]{2,1,0:T(8,128)(2,1)}, u32[]{:S(2)}) copy-start(bf16[2,128,2048]{2,1,0:T(8,128)(2,1)} %param.16) | copy-start | bytes 3145732
  96.2 96.0 %all-gather.4.cloned.1.call-start = ((), (), s32[]{:S(2)}) async-start(), calls=%async_computation.2 | async-start | bytes 6488064 | tf_op jit(solution)/shard_map/all_gather | solution.py:134
  96.8 187.8 %all-gather.6.cloned.1.call-start = ((), (), s32[]{:S(2)}) async-start(), calls=%async_computation.3 | async-start | bytes 6488064 | tf_op jit(solution)/shard_map/all_gather | solution.py:139
  97.4 94.9 %copy-start.7 = (f32[2048]{0:T(1024)S(1)}, f32[2048]{0:T(1024)}, u32[]{:S(2)}) copy-start(f32[2048]{0:T(1024)} %param.25) | copy-start | bytes 24580
  97.4 279.5 %all-gather.8.cloned.1.call-start = ((), (), s32[]{:S(2)}) async-start(), calls=%async_computation.4 | async-start | bytes 6488064 | tf_op jit(solution)/shard_map/all_gather | solution.py:145
  97.9 311.6 %reduce-scatter.2.cloned.1.call-start = ((), (), s32[]{:S(2)}) async-start(), calls=%async_computation.5 | async-start | bytes 1310720 | tf_op jit(solution)/shard_map/reduce_scatter | solution.py:149
  386.4 30.7 %copy-start.5 = (s32[2]{0:T(128)S(1)}, s32[2]{0:T(128)}, u32[]{:S(2)}) copy-start(s32[2]{0:T(128)} %param.29) | copy-start | bytes 28
Sparse Core Ops, SparseCore 0:
  96.3 37.7 all-reduce.2
  386.6 22.9 reduce-scatter.1
Sparse Core Ops, SparseCore 1:
  98.9 93.3 all-gather.3
  194.3 90.2 all-gather.5
  286.6 90.2 all-gather.7
where the time goes:
time: 448 us; the launch traced here: 447 us
  waiting for transfers between devices  295 us (66%)
  blocking collectives  95.7 us (21%)
  matrix products  22.6 us (5%)
  between operations  15.9 us (4%)
  other arithmetic  15.5 us (3%)
    all_gather x1, waiting for transfers between devices, local(): lax.all_gather(down_weight, 'seq', axis=0, tiled=True)  92.4 us
    all_gather x1, waiting for transfers between devices, local(): lax.all_gather(up_weight, 'seq', axis=0, tiled=True)  86.4 us
    all_gather x1, waiting for transfers between devices, local(): lax.all_gather(gate_weight, 'seq', axis=0, tiled=True)  55.5 us
    psum x1, waiting for transfers between devices, local(): summed = lax.psum(projected.astype(jnp.bfloat16), 'mp').astype(jnp.float32)  35.9 us
    all_gather x1, blocking collectives, local(): key_piece = lax.all_gather(rotated_k, 'seq', axis=1, tiled=True)  35.3 us
    all_gather x1, blocking collectives, local(): value_piece = lax.all_gather(value_rows, 'seq', axis=1, tiled=True)  33.2 us
    reduce_scatter x1, waiting for transfers between devices, local(): lax.psum_scatter(down_part.astype(jnp.bfloat16), 'mp', scatter_dimension=...  23.1 us
    psum x1, blocking collectives, local(): seq_total = lax.psum(jnp.sum(influence, axis=1), 'seq')  21.5 us
  transfers between devices with their start and end apart: 5, of which 5 were waited for; matrix products, arithmetic and copies ran while one was open for 2% of the time, Pallas kernels for 0%

commit v1 on v0

--- a/solution.py
+++ b/solution.py
@@ -2,6 +2,7 @@
 import jax.numpy as jnp
 from jax import lax
 from jax.sharding import PartitionSpec as P
+from jax.lax import all_gather
 
 HEADS = 16
 KV_HEADS = 2
@@ -105,7 +106,7 @@
     )
     key_start = jnp.int32(0)
     key_piece = lax.all_gather(rotated_k, "seq", axis=1, tiled=True)
-    value_piece = lax.all_gather(value_rows, "seq", axis=1, tiled=True)
+    value_piece = jnp.concatenate(all_gather(value_rows, "seq"), axis=1)
     updated = []
     for state, query_entry in zip(initial, query_sets):
         queries, first_pos = query_entry

time: 448 us -> 448 us (level)
  no operation moved by 1% of the time
where the time goes in v1:
time: 448 us; the launch traced here: 447 us
  waiting for transfers between devices  295 us (66%)
  blocking collectives  95.7 us (21%)
  matrix products  22.6 us (5%)
  between operations  15.9 us (4%)
  other arithmetic  15.5 us (3%)
    all_gather x1, waiting for transfers between devices, local(): lax.all_gather(down_weight, 'seq', axis=0, tiled=True)  92.4 us
    all_gather x1, waiting for transfers between devices, local(): lax.all_gather(up_weight, 'seq', axis=0, tiled=True)  86.4 us
    all_gather x1, waiting for transfers between devices, local(): lax.all_gather(gate_weight, 'seq', axis=0, tiled=True)  55.5 us
    psum x1, waiting for transfers between devices, local(): summed = lax.psum(projected.astype(jnp.bfloat16), 'mp').astype(jnp.float32)  35.9 us
    all_gather x1, blocking collectives, local(): key_piece = lax.all_gather(rotated_k, 'seq', axis=1, tiled=True)  35.3 us
    all_gather x1, blocking collectives, local(): value_piece = jnp.concatenate(all_gather(value_rows, 'seq'), axis=1)  33.2 us
    reduce_scatter x1, waiting for transfers between devices, local(): lax.psum_scatter(down_part.astype(jnp.bfloat16), 'mp', scatter_dimension=...  23.1 us
    psum x1, blocking collectives, local(): seq_total = lax.psum(jnp.sum(influence, axis=1), 'seq')  21.5 us
  transfers between devices with their start and end apart: 5, of which 5 were waited for; matrix products, arithmetic and copies ran while one was open for 2% of the time, Pallas kernels for 0%

profile of v1, /device:TPU:0, one launch (start us, length us, event | category | flops | bytes accessed | tf_op | source)
XLA Modules:
  0.0 447.5 jit_solution(15365693983427392160)
XLA Ops:
  8.0 0.0 copy-start
  8.0 0.0 all-reduce.3.cloned.1.call-start
  8.1 1.6 multiply_reduce_fusion
  9.8 0.0 copy-start.4
  9.8 0.8 dynamic_slice.19
  10.6 1.5 fusion.13
  12.2 0.0 copy-done.4
  12.2 0.0 copy-start.9
  12.2 0.4 convolution_add_fusion.2
  12.6 0.0 copy-start.8
  12.6 0.7 slice_negate_fusion.1
  13.3 0.1 broadcast_multiply_fusion
  13.4 0.3 fusion.35
  13.8 1.2 fusion.33
  15.0 35.3 %all_gather.15 = bf16[2,1024,128]{2,1,0:T(8,128)(2,1)} all-gather(bf16[2,128,128]{2,1,0:T(8,128)(2,1)S(1)} %fusion.33), channel_id=1, replica_groups=mesh['seq'=8,'mp'=4] {'seq'}, dimensions={1}, use_global_device_ids=true | all-gather | bytes 589824 | tf_op jit(solution)/shard_map/all_gather | solution.py:108
  50.2 0.0 copy-done.9
  50.2 0.1 dynamic_slice.21
  50.3 1.5 fusion.18
  51.8 33.2 %all_gather.16 = bf16[8,2,128,128]{3,2,0,1:T(8,128)(2,1)} all-gather(bf16[1,2,128,128]{3,2,0,1:T(8,128)(2,1)S(1)} %bitcast.55), channel_id=1, replica_groups=mesh['seq'=8,'mp'=4] {'seq'}, dimensions={0}, use_global_device_ids=true | all-gather | bytes 589824 | tf_op jit(solution)/shard_map/all_gather | solution.py:109
  85.0 0.0 copy-done.8
  85.0 0.0 copy-done.6
  85.0 1.5 convolution_add_fusion
  86.5 1.2 reshape.198
  87.8 0.0 copy-start.2
  87.8 1.2 slice_negate_fusion
  88.9 1.4 fusion.22
  90.4 0.0 copy-done.2
  90.4 3.7 conditional.1
  90.4 0.1 iota_compare_fusion
  90.5 0.0 copy-start.3
  90.5 0.9 fusion
  91.5 0.1 copy-done.3
  91.6 1.1 fusion.3
  92.7 1.3 fusion.2
  94.0 0.2 fusion.31
  94.3 0.2 copy.21
  94.5 0.0 copy-done
  94.5 1.7 convolution_convert_fusion
  96.2 0.0 all-reduce.3.cloned.1.call-update
  96.2 0.0 all-gather.4.cloned.1.call-start
  96.2 0.5 all-gather.4.cloned.1.call-update
  96.8 0.0 all-gather.6.cloned.1.call-start
  96.8 0.5 all-gather.6.cloned.1.call-update
  97.4 0.0 copy-start.7
  97.4 0.0 all-gather.8.cloned.1.call-start
  97.4 0.5 all-gather.8.cloned.1.call-update
  97.9 0.2 reduce-scatter.2.cloned.1.call-start
  98.2 35.9 %all-reduce.3.cloned.1.call-done = bf16[256,2048]{1,0:T(8,128)(2,1)} async-done(((bf16[256,2048]{1,0:T(8,128)(2,1)}), bf16[256,2048]{1,0:T(8,128)(2,1)}) %all-reduce.3.cloned.1.call-update) | async-done | bytes 1048592 | tf_op jit(solution)/shard_map/psum | solution.py:129
  134.1 0.0 copy-done.1
  134.1 2.6 fusion.15
  136.7 55.5 %all-gather.4.cloned.1.call-done = bf16[2048,1408]{1,0:T(8,128)(2,1)} async-done(((bf16[256,1408]{1,0:T(8,128)(2,1)}), bf16[2048,1408]{1,0:T(8,128)(2,1)}) %all-gather.4.cloned.1.call-update) | async-done | bytes 5767184 | tf_op jit(solution)/shard_map/all_gather | solution.py:135
  192.2 0.0 copy-done.7
  192.2 6.0 %fusion.27 = f32[256,1408]{1,0:T(8,128)} fusion(bf16[2048,1408]{1,0:T(8,128)(2,1)} %all-gather.4.cloned.1.call-done, bf16[256,2048]{1,0:T(8,128)(2,1)} %get-tuple-element.28, f32[2048]{0:T(1024)S(1)} %copy-done.7, f32[256]{0:T(256)S(1)} %add_rsqrt_fusion), kind=kOutput, calls=%fused_computation.47 | convolution fusion | flops 1478492160 | bytes 8266752 | tf_op jit(solution)/shard_map/dot_general | solution.py:133
  198.2 86.4 %all-gather.6.cloned.1.call-done = bf16[2048,1408]{1,0:T(8,128)(2,1)} async-done(((bf16[256,1408]{1,0:T(8,128)(2,1)}), bf16[2048,1408]{1,0:T(8,128)(2,1)}) %all-gather.6.cloned.1.call-update) | async-done | bytes 5767184 | tf_op jit(solution)/shard_map/all_gather | solution.py:140
  284.6 92.4 %all-gather.8.cloned.1.call-done = bf16[2048,1408]{1,0:T(8,128)(2,1)} async-done(((bf16[256,1408]{1,0:T(8,128)(2,1)}), bf16[2048,1408]{1,0:T(8,128)(2,1)}) %all-gather.8.cloned.1.call-update) | async-done | bytes 5767184 | tf_op jit(solution)/shard_map/all_gather | solution.py:146
  376.9 9.5 %convolution_convert_fusion.1 = bf16[256,2048]{1,0:T(8,128)(2,1)} fusion(bf16[2048,1408]{1,0:T(8,128)(2,1)} %all-gather.8.cloned.1.call-done, bf16[2048,1408]{1,0:T(8,128)(2,1)} %all-gather.6.cloned.1.call-done, f32[256,1408]{1,0:T(8,128)} %fusion.27, bf16[256,2048]{1,0:T(8,128)(2,1)} %get-tuple-element.28, f32[2048]{0:T(1024)S(1)} %copy-done.7, ...), kind=kOutput, calls=%fused_computation.22 | convolution fusion | flops 2957574144 | bytes 15082496 | tf_op jit(solution)/shard_map/dot_general | solution.py:144
  386.4 0.0 reduce-scatter.2.cloned.1.call-update
  386.5 23.1 %reduce-scatter.2.cloned.1.call-done = bf16[256,512]{1,0:T(8,128)(2,1)} async-done(((bf16[256,2048]{1,0:T(8,128)(2,1)}), bf16[256,512]{1,0:T(8,128)(2,1)}) %reduce-scatter.2.cloned.1.call-update) | async-done | bytes 262160 | tf_op jit(solution)/shard_map/reduce_scatter | solution.py:150
  409.5 1.8 fusion.20
  411.4 5.7 %all-reduce = (f32[2,128]{1,0:T(2,128)S(1)}, f32[2,128]{1,0:T(2,128)S(1)}) all-reduce(f32[2,128]{1,0:T(2,128)S(1)} %bitcast.58, f32[2,128]{1,0:T(2,128)S(1)} %bitcast.57), channel_id=1, replica_groups=mesh['seq'=8,'mp'=4] {'mp'}, use_global_device_ids=true, to_apply=%region_9.10 | all-reduce | flops 512 | bytes 4096 | tf_op jit(solution)/shard_map/psum | solution.py:158
  417.1 0.0 copy-done.5
  417.1 0.7 fusion.40
  417.8 21.5 %psum.31 = f32[2]{0:T(128)S(1)} all-reduce(f32[2]{0:T(128)S(1)} %get-tuple-element.24), channel_id=1, replica_groups=mesh['seq'=8,'mp'=4] {'seq'}, use_global_device_ids=true, to_apply=%region_13.14 | all-reduce | flops 2 | bytes 16 | tf_op jit(solution)/shard_map/psum | solution.py:164
  439.4 0.5 convert_divide_fusion
  (11 shorter events, 0.1 us)
Async XLA Ops:
  8.0 86.5 %copy-start = (bf16[512,2048]{1,0:T(8,128)(2,1)S(1)}, bf16[512,2048]{1,0:T(8,128)(2,1)}, u32[]{:S(2)}) copy-start(bf16[512,2048]{1,0:T(8,128)(2,1)} %param.24) | copy-start | bytes 6291460
  8.0 126.1 %all-reduce.3.cloned.1.call-start = ((), (), s32[]{:S(2)}) async-start(), calls=%async_computation.1 | async-start | bytes 2097152 | tf_op jit(solution)/shard_map/psum | solution.py:129
  9.8 2.4 copy-start.4
  12.2 38.1 %copy-start.9 = (f32[256]{0:T(256)S(1)}, f32[256]{0:T(256)}, u32[]{:S(2)}) copy-start(f32[256]{0:T(256)} %param.23) | copy-start | bytes 3076
  12.6 72.4 %copy-start.8 = (f32[512]{0:T(512)S(1)}, f32[512]{0:T(512)}, u32[]{:S(2)}) copy-start(f32[512]{0:T(512)} %param.19) | copy-start | bytes 6148
  13.3 71.7 %copy-start.6 = (bf16[2048,512]{1,0:T(8,128)(2,1)S(1)}, bf16[2048,512]{1,0:T(8,128)(2,1)}, u32[]{:S(2)}) copy-start(bf16[2048,512]{1,0:T(8,128)(2,1)} %param.18) | copy-start | bytes 6291460
  87.8 2.6 copy-start.2
  90.5 1.0 copy-start.3
  96.2 38.0 %copy-start.1 = (bf16[2,128,2048]{2,1,0:T(8,128)(2,1)S(1)}, bf16[2,128,2048]{2,1,0:T(8,128)(2,1)}, u32[]{:S(2)}) copy-start(bf16[2,128,2048]{2,1,0:T(8,128)(2,1)} %param.16) | copy-start | bytes 3145732
  96.2 96.0 %all-gather.4.cloned.1.call-start = ((), (), s32[]{:S(2)}) async-start(), calls=%async_computation.2 | async-start | bytes 6488064 | tf_op jit(solution)/shard_map/all_gather | solution.py:135
  96.8 187.8 %all-gather.6.cloned.1.call-start = ((), (), s32[]{:S(2)}) async-start(), calls=%async_computation.3 | async-start | bytes 6488064 | tf_op jit(solution)/shard_map/all_gather | solution.py:140
  97.4 94.9 %copy-start.7 = (f32[2048]{0:T(1024)S(1)}, f32[2048]{0:T(1024)}, u32[]{:S(2)}) copy-start(f32[2048]{0:T(1024)} %param.25) | copy-start | bytes 24580
  97.4 279.5 %all-gather.8.cloned.1.call-start = ((), (), s32[]{:S(2)}) async-start(), calls=%async_computation.4 | async-start | bytes 6488064 | tf_op jit(solution)/shard_map/all_gather | solution.py:146
  97.9 311.6 %reduce-scatter.2.cloned.1.call-start = ((), (), s32[]{:S(2)}) async-start(), calls=%async_computation.5 | async-start | bytes 1310720 | tf_op jit(solution)/shard_map/reduce_scatter | solution.py:150
  386.4 30.7 %copy-start.5 = (s32[2]{0:T(128)S(1)}, s32[2]{0:T(128)}, u32[]{:S(2)}) copy-start(s32[2]{0:T(128)} %param.29) | copy-start | bytes 28
Sparse Core Ops, SparseCore 0:
  96.3 37.7 all-reduce.2
  386.6 22.9 reduce-scatter.1
Sparse Core Ops, SparseCore 1:
  98.9 93.3 all-gather.3
  194.3 90.2 all-gather.5
  286.6 90.2 all-gather.7
